TPU v7x, 256 devices: a 2x2x32 block of a 4x8x32 slice. The times are simulated.
256 devices in a mesh: field: 4 (over y, x), ep: 64 (over z, core).
Axes of the slice: x: 2, y: 2, z: 32, core: 2. Of those that a mesh axis runs over, the one named last changes fastest.
The devices are a block of a 4x8x32 slice.
Arguments:
- images: float32 [512, 64, 256], P(('field', 'ep')), parts along dimension 0, may hold values from -6 to 6
- reference_image: float32 [256, 256], P('field'), parts along dimension 0, may hold values from -6 to 6
- kernels: float32 [16, 23, 23], replicated, may hold values from -0.25 to 0.25
- kernel_index: int32 [512], P(('field', 'ep')), parts along dimension 0, may hold values from 0 to 15
- tile_mask: int32 [512, 64, 2], P(('field', 'ep')), parts along dimension 0, may hold values 0 or 1
- systematics: float32 [512, 40], P('field'), parts along dimension 0, may hold values from -6 to 6
- onsets: int32 [32], P('field'), parts along dimension 0, may hold values from 0 to 123
Outputs:
- coefficients: float32 [48, 256, 256], P(None, ('field', 'ep')), parts along dimension 1
- epoch_scatter: float32 [512], P('field'), parts along dimension 0
There are 4 independent parts, one for each index of `field`. A program takes and returns all parts, laid end to end along the dimension named above; an argument that names none is the same for every part. Nothing has to cross between parts.
All inputs are finite; a program needn't handle non-finite values. No bound on the sum of `tile_mask` on one device may be relied on, other than what follows from the above.
Results may differ from a plain program's by a relative error of at most 0.00011.
Values sent between devices are 32-bit elements; how exact they have to be, the bound alone decides.
A program may use at most 64 MiB of HBM per device.

v0:
```python
import math

import jax
import jax.numpy as jnp
from jax import lax
from jax.sharding import PartitionSpec as P

cov_ridge = 0.5
fit_ridge = 1.0


def gathered_total(value, axis):
    return lax.all_gather(value, axis).sum(0)


def correlate(stack, chosen):
    count, rows, width = stack.shape
    side = chosen.shape[1]
    half = (side - 1) // 2
    padded = jnp.pad(stack, ((0, 0), (half, half), (half, half)))
    filters = jnp.transpose(chosen, (1, 2, 0))[:, :, None, :]
    strip = math.gcd(rows, 16)

    def one_strip(start):
        piece = lax.dynamic_slice_in_dim(padded, start, strip + 2 * half, 1)
        result = lax.conv_general_dilated(
            piece[None],
            filters,
            (1, 1),
            "VALID",
            dimension_numbers=("NCHW", "HWIO", "NCHW"),
            feature_group_count=count,
            precision=lax.Precision.HIGHEST,
        )
        return result[0]

    starts = jnp.arange(rows // strip, dtype=jnp.int32) * strip
    strips = lax.map(one_strip, starts)
    return jnp.transpose(strips, (1, 0, 2, 3)).reshape(count, rows, width)


def subtract(stack, reference_image, chosen, masks):
    result = reference_image[None] - correlate(stack, chosen)
    shape = result.shape
    tiles = result.reshape(shape[0], shape[1], shape[2] // 128, 128) * masks[..., None].astype(
        jnp.float32
    )
    return tiles.reshape(shape)


def build_design(systematics, onsets):
    count = systematics.shape[0]
    templates = onsets.shape[0]
    epoch_axis = jnp.arange(count, dtype=jnp.float32)[:, None]
    delays = epoch_axis - onsets[None, :].astype(jnp.float32)
    timescale = (jnp.arange(templates, dtype=jnp.float32) + 1.0) * count / (2.0 * templates)
    transient = jnp.where(
        delays >= 0.0, jnp.exp(-jnp.maximum(delays, 0.0) / timescale[None, :]), 0.0
    )
    return jnp.concatenate([systematics, transient], axis=1)


def fit_matrix(scatter, npixels, design):
    count = design.shape[0]
    columns = design.shape[1]
    covariance = scatter / npixels + cov_ridge * jnp.eye(count, dtype=scatter.dtype)
    lower = jnp.linalg.cholesky(covariance)
    weighted = jax.scipy.linalg.cho_solve((lower, True), design)
    normal = jnp.dot(design.T, weighted, precision=lax.Precision.HIGHEST) + fit_ridge * jnp.eye(
        columns, dtype=scatter.dtype
    )
    lower_fit = jnp.linalg.cholesky(normal)
    return jax.scipy.linalg.cho_solve((lower_fit, True), weighted.T)


def shards(images, reference_image, kernels, kernel_index, tile_mask, systematics, onsets):
    local_count, rows, width = images.shape
    basis = kernels.shape[0]
    side = kernels.shape[1]
    onehot = (kernel_index[:, None] == jnp.arange(basis, dtype=jnp.int32)[None, :]).astype(
        jnp.float32
    )
    chosen = jnp.dot(
        onehot, kernels.reshape(basis, side * side), precision=lax.Precision.HIGHEST
    ).reshape(local_count, side, side)
    difference = subtract(images, reference_image, chosen, tile_mask)
    received = lax.all_to_all(difference, "ep", split_axis=1, concat_axis=0, tiled=True)
    count = received.shape[0]
    block_rows = received.shape[1]
    pixel_data = received.reshape(count, block_rows * width)
    partial_value = jnp.dot(pixel_data, pixel_data.T, precision=lax.Precision.HIGHEST)
    scatter = gathered_total(partial_value, "ep")
    npixels = float(rows * width)
    design = build_design(systematics, onsets)
    fit = fit_matrix(scatter, npixels, design)
    coefficients = jnp.dot(fit, pixel_data, precision=lax.Precision.HIGHEST)
    projector = jnp.eye(count, dtype=jnp.float32) - jnp.dot(
        design, fit, precision=lax.Precision.HIGHEST
    )
    product = jnp.dot(projector, scatter, precision=lax.Precision.HIGHEST)
    epoch_scatter = jnp.sum(product * projector, axis=1) / npixels
    return (coefficients.reshape(design.shape[1], block_rows, width), epoch_scatter)


def solution(mesh):
    in_specs = (
        P(("field", "ep"), None, None),
        P("field", None),
        P(),
        P(("field", "ep")),
        P(("field", "ep"), None, None),
        P("field", None),
        P("field"),
    )
    out_specs = (P(None, ("field", "ep"), None), P("field"))
    return jax.shard_map(shards, mesh=mesh, in_specs=in_specs, out_specs=out_specs, check_vma=False)
```

profile of v0, /device:TPU:37, one launch (start us, length us, event | category | flops | bytes accessed | tf_op | source)
XLA Modules:
  0.0 700.7 jit_solution(15201443490369932279)
XLA Ops:
  7.8 1.0 copy.49
  10.2 1.7 pad.4
  11.9 459.0 %while.10 = (s32[]{:T(128)}, f32[4,2,16,256]{3,2,0,1:T(8,128)}, s32[4]{0:T(128)}, f32[2,86,278]{2,1,0:T(8,128)}, f32[23,23,1,2]{3,2,1,0:T(1,128)S(1)}, /*index=5...) while((s32[]{:T(128)}, f32[4,2,16,256]{3,2,0,1:T(8,128)}, s32[4]{0:T(128)}, ...), condition=%wide.region_1.2_spmd, body=%wide.region_0.1_spmd.sunk | while | flops 56991012 | bytes 1433015 | solution.py:38
  11.9 1.3 dynamic_slice.11
  15.1 0.9 dynamic-slice_bitcast_fusion.2
  17.0 0.9 slice.46
  17.9 1.1 fusion.64
  19.1 106.6 %fusion.65 = f32[16,8,35,2]{1,3,2,0:T(2,128)S(1)} fusion(f32[23,23,1,2]{3,2,1,0:T(1,128)S(1)} %get-tuple-element.123, pred[8,35]{0,1:T(8,128)(4,1)S(1)} %copy-done.4, f32[2,38,8,57]{2,0,3,1:T(2,128)S(1)} %fusion.64), kind=kOutput, calls=%fused_computation.6.clone.2 | convolution fusion | flops 56887040 | bytes 178976 | tf_op jit(solution)/shard_map/while/body/eval_jaxpr/conv_general_dilated | solution.py:26
  126.7 1.2 dynamic_slice.11
  129.8 0.9 dynamic-slice_bitcast_fusion.2
  131.7 0.9 slice.46
  132.7 1.1 fusion.64
  133.8 106.6 %fusion.65 = f32[16,8,35,2]{1,3,2,0:T(2,128)S(1)} fusion(f32[23,23,1,2]{3,2,1,0:T(1,128)S(1)} %get-tuple-element.123, pred[8,35]{0,1:T(8,128)(4,1)S(1)} %copy-done.4, f32[2,38,8,57]{2,0,3,1:T(2,128)S(1)} %fusion.64), kind=kOutput, calls=%fused_computation.6.clone.2 | convolution fusion | flops 56887040 | bytes 178976 | tf_op jit(solution)/shard_map/while/body/eval_jaxpr/conv_general_dilated | solution.py:26
  241.4 1.2 dynamic_slice.11
  244.6 0.9 dynamic-slice_bitcast_fusion.2
  246.5 0.9 slice.46
  247.4 1.1 fusion.64
  248.6 106.6 %fusion.65 = f32[16,8,35,2]{1,3,2,0:T(2,128)S(1)} fusion(f32[23,23,1,2]{3,2,1,0:T(1,128)S(1)} %get-tuple-element.123, pred[8,35]{0,1:T(8,128)(4,1)S(1)} %copy-done.4, f32[2,38,8,57]{2,0,3,1:T(2,128)S(1)} %fusion.64), kind=kOutput, calls=%fused_computation.6.clone.2 | convolution fusion | flops 56887040 | bytes 178976 | tf_op jit(solution)/shard_map/while/body/eval_jaxpr/conv_general_dilated | solution.py:26
  356.2 1.2 dynamic_slice.11
  359.3 0.9 dynamic-slice_bitcast_fusion.2
  361.2 0.9 slice.46
  362.2 1.1 fusion.64
  363.3 106.6 %fusion.65 = f32[16,8,35,2]{1,3,2,0:T(2,128)S(1)} fusion(f32[23,23,1,2]{3,2,1,0:T(1,128)S(1)} %get-tuple-element.123, pred[8,35]{0,1:T(8,128)(4,1)S(1)} %copy-done.4, f32[2,38,8,57]{2,0,3,1:T(2,128)S(1)} %fusion.64), kind=kOutput, calls=%fused_computation.6.clone.2 | convolution fusion | flops 56887040 | bytes 178976 | tf_op jit(solution)/shard_map/while/body/eval_jaxpr/conv_general_dilated | solution.py:26
  471.4 0.9 fusion.15
  472.4 64.2 %all_to_all.15 = f32[2,64,256]{2,0,1:T(2,128)S(1)} all-to-all(f32[2,64,256]{2,0,1:T(2,128)S(1)} %copy.54), channel_id=1, replica_groups=mesh['field'=4,'ep'=64] {'ep'}, dimensions={1} | all-to-all | bytes 262144 | tf_op jit(solution)/shard_map/all_to_all | solution.py:87
  536.7 0.9 fusion.39
  537.8 118.1 %all-gather.3.cloned.1.call-done = f32[8192,128]{1,0:T(8,128)} async-done(((f32[128,128]{1,0:T(8,128)}), f32[8192,128]{1,0:T(8,128)}) %all-gather.3.cloned.1.call-update) | async-done | bytes 4194320 | tf_op jit(solution)/shard_map/all_gather | solution.py:13
  655.9 2.4 reduce_sum.18
  658.5 11.7 %cholesky.34 = f32[128,128]{1,0:T(8,128)S(1)} custom-call(f32[128,128]{1,0:T(8,128)S(1)} %fusion.22), custom_call_target="Cholesky" | custom-call | tf_op jit(solution)/shard_map/jit(cholesky)/cholesky | solution.py:67
  671.6 9.8 %custom-call.20 = f32[1,128,128]{1,2,0:T(8,128)S(1)} custom-call(f32[1,128,128]{2,1,0:T(8,128)S(1)} %fusion.16), custom_call_target="InvertDiagBlocksLowerTriangular" | custom-call | tf_op jit(solution)/shard_map/jit(_cho_solve)/triangular_solve | solution.py:68
  682.1 4.4 cholesky.64
  687.8 3.7 custom-call.21
  (79 shorter events, 16.5 us)
Async XLA Ops:
  7.2 648.7 %all-gather.3.cloned.1.call-start = ((), (), s32[]{:S(2)}) async-start(), calls=%async_computation.1 | async-start | bytes 4259840 | tf_op jit(solution)/shard_map/all_gather | solution.py:13
  11.9 459.0 %copy-start.2 = (s32[2,64,2]{1,2,0:T(2,128)S(1)}, s32[2,64,2]{1,2,0:T(2,128)}, u32[]{:S(2)}) copy-start(s32[2,64,2]{1,2,0:T(2,128)} %param.13) | copy-start | bytes 3076
  11.9 459.5 %copy-start.1 = (f32[64,256]{1,0:T(8,128)S(1)}, f32[64,256]{1,0:T(8,128)}, u32[]{:S(2)}) copy-start(f32[64,256]{1,0:T(8,128)} %param.10) | copy-start | bytes 196612
  11.9 525.7 %copy-start.3 = (s32[8]{0:T(128)S(1)}, s32[8]{0:T(128)}, u32[]{:S(2)}) copy-start(s32[8]{0:T(128)} %param.15) | copy-start | bytes 100
  17.9 1.1 copy-start.4
  132.7 1.1 copy-start.4
  247.4 1.1 copy-start.4
  362.2 1.1 copy-start.4
  655.9 25.5 %copy-start = (f32[128,40]{0,1:T(8,128)S(1)}, f32[128,40]{0,1:T(8,128)}, u32[]{:S(2)}) copy-start(f32[128,40]{0,1:T(8,128)} %param.14) | copy-start | bytes 61444
Sparse Core Ops, SparseCore 0:
  537.8 118.0 all-gather.2
where the time goes:
time: 701 us
  matrix products  430 us (61%)
  waiting for transfers between devices  118 us (17%)
  blocking collectives  64.2 us (9%)
  other arithmetic  41.2 us (6%)
  local copies, waits for them, and re-layouts  25.1 us (4%)
  between operations  14.3 us (2%)
  loops' own time  7.76 us (1%)
    conv_general_dilated x4, matrix products, one_strip(): lax.conv_general_dilated(piece[None], filters, (1, 1), 'VALID', dimension...  426 us
    all_gather x1, waiting for transfers between devices, gathered_total(): return lax.all_gather(value, axis).sum(0)  118 us
    all_to_all x1, blocking collectives, shards(): lax.all_to_all(difference, 'ep', split_axis=1, concat_axis=0, tiled=True)  64.2 us
  transfers between devices with their start and end apart: 1, of which 1 were waited for; matrix products, arithmetic and copies ran while one was open for 0% of the time, Pallas kernels for 0%

commit v1 on v0

v1 whole, which is shorter than its diff:
```python
import functools

import jax
import jax.numpy as jnp
from jax import lax
from jax.experimental import pallas as pl
from jax.experimental.pallas import tpu as pltpu
from jax.sharding import PartitionSpec as P

f32, bf16, i32 = jnp.float32, jnp.bfloat16, jnp.int32
HIGHEST = lax.Precision.HIGHEST
cov_ridge = 0.5
LANES = 128


def split(x):
    high = x.astype(bf16).astype(f32)
    return high, x - high


def iota(shape, axis):
    return lax.broadcasted_iota(i32, shape, axis)


def correlate(image, kernel, kpad, bands, shifted):
    side = kernel.shape[0]
    half = side // 2
    rows = image.shape[0]
    kpad[...] = jnp.zeros_like(kpad)
    kpad[0:side, 0:side] = kernel
    high, low = split(kpad[...].T)
    base = pltpu.roll(high, LANES - half, 1) + pltpu.roll(low, rows - half, 1)
    lane = iota((rows, LANES), 1)
    band = jnp.abs(lax.rem(lane, rows) - iota((rows, LANES), 0)) <= half
    for b in range(side):
        column = jnp.broadcast_to(base[b : b + 1, :], (rows, LANES))
        column = pltpu.roll(column, 0, 1, stride=1, stride_axis=0)
        bands[b * rows : (b + 1) * rows, :] = jnp.where(band, column, 0.0).astype(bf16)
    high, low = split(image)
    high, low = high.astype(bf16), low.astype(bf16)
    left = bands[...]
    shifted[...] = jnp.dot(
        jnp.concatenate([left, left], axis=1),
        jnp.concatenate([high, high, low, low], axis=0),
        preferred_element_type=f32,
    )
    total = [None, None]
    for b in range(side):
        s = b - half
        block = slice(b * rows, (b + 1) * rows)
        first, second = shifted[block, 0:LANES], shifted[block, LANES:]
        if s:
            x = pltpu.roll(first, (-s) % LANES, 1)
            y = pltpu.roll(second, (-s) % LANES, 1)
            if s > 0:
                inside = lane < LANES - s
                first, second = jnp.where(inside, x, y), jnp.where(inside, y, 0.0)
            else:
                inside = lane >= -s
                first, second = jnp.where(inside, x, 0.0), jnp.where(inside, y, x)
        total = [v if t is None else t + v for t, v in zip(total, (first, second))]
    return total


def eliminate(matrix, right):
    count = matrix.shape[0]
    width = 8
    row8 = iota((width, LANES), 0)
    for k in range(0, count, width):
        pivot = slice(k, k + width)
        columns = [
            jnp.broadcast_to(matrix[:, k + j : k + j + 1], (count, LANES)) for j in range(width)
        ]
        block = [c[pivot, :] for c in columns]
        a, x = matrix[pivot, :], right[pivot, :]
        for j in range(width):
            factor = block[j]
            inverse = 1.0 / factor[j : j + 1, :]

            def step(v):
                scaled = v[j : j + 1, :] * inverse
                return jnp.where(row8 == j, scaled, v - factor * scaled)

            a, x = step(a), step(x)
            for m in range(j + 1, width):
                block[m] = step(block[m])

        def update(value, rows):
            for j in range(width):
                value = value - columns[j] * rows[j : j + 1, :]
            above = [value[:k, :]] if k else []
            below = [value[k + width :, :]] if k + width < count else []
            return jnp.concatenate([*above, rows, *below], axis=0)

        if k + width < count:
            matrix = update(matrix, a)
        right = update(right, x)
    return right


def body(
    devices,
    index_ref,
    onsets_ref,
    images_ref,
    reference_ref,
    kernels_ref,
    mask_ref,
    systematics_ref,
    coefficients_ref,
    scatter_ref,
    kpad,
    bands,
    shifted,
    parcel,
    inbox,
    pair_box,
    half_sum,
    gathered,
    fit_ref,
    spare,
    residual_ref,
    design_ref,
    sems,
    fit_send,
    fit_got,
    residual_send,
    residual_got,
):
    local, rows, width = images_ref.shape
    owners = devices // 2
    me = lax.axis_index("ep")
    core = lax.rem(me, 2)
    partner = me + 1 - 2 * core
    root = 1
    epochs = systematics_ref.shape[0]
    pixels = float(rows * width)

    def remote(source, target, sems, device):
        send, receive = sems
        return pltpu.make_async_remote_copy(
            src_ref=source,
            dst_ref=target,
            send_sem=send,
            recv_sem=receive,
            device_id={"ep": device},
        )

    parcel_sems, pair_sems, gather_sems, row_sems = (
        (sems.at[2 * i], sems.at[2 * i + 1]) for i in range(4)
    )

    is_owner = me < owners
    barrier = pltpu.get_barrier_semaphore()

    @pl.when(is_owner)
    def _():
        @pl.loop(1, devices)
        def _(step):
            pl.semaphore_signal(barrier, inc=1, device_id={"ep": lax.rem(me + step, devices)})

    for e in range(local):
        conv = correlate(
            images_ref[e], kernels_ref[:, index_ref[e], :], kpad.at[e], bands.at[e], shifted.at[e]
        )
        for t in range(width // LANES):
            lanes = slice(t * LANES, (t + 1) * LANES)
            good = jnp.broadcast_to(mask_ref[e, :, t : t + 1].astype(f32), (rows, LANES))
            difference = (reference_ref[:, lanes] - conv[t]) * good
            for k in range(2):
                parcel[pl.ds(k * 4 + t * 2 + e, owners, stride=8), :] = difference[
                    k * owners : (k + 1) * owners, :
                ]

    @pl.when(is_owner)
    def _():
        pl.semaphore_wait(barrier, owners - 1)

    @pl.when(jnp.logical_not(is_owner))
    def _():
        pl.semaphore_wait(barrier, owners)

    def tile(ref, index):
        return ref.at[pl.ds(pl.multiple_of(index * 8, 8), 8), :]

    def send_to(owner):
        @pl.when(owner != me)
        def _():
            remote(tile(parcel, owner), tile(inbox, me), parcel_sems, owner).start()

    @pl.loop(0, owners)
    def _(step):
        send_to(owners - 1 - step)

    @pl.when(is_owner)
    def _():
        inbox[pl.ds(pl.multiple_of(me * 8, 8), 8), :] = parcel[
            pl.ds(pl.multiple_of(me * 8, 8), 8), :
        ]
        arrived = inbox.at[pl.ds(0, (devices - 1) * 8), :]
        remote(arrived, arrived, parcel_sems, partner).wait_recv()
        sent = parcel.at[pl.ds(0, (owners - 1) * 8), :]
        remote(sent, sent, parcel_sems, partner).wait_send()

    @pl.when(jnp.logical_not(is_owner))
    def _():
        remote(parcel, parcel, parcel_sems, partner).wait_send()

    def order(ref_rows):
        return [ref_rows(h, e) for h in range(2) for e in range(local)]

    def data(k, t):
        return jnp.concatenate(
            order(
                lambda h, e: inbox[
                    pl.ds(h * owners * 8 + k * 4 + t * 2 + e, owners, stride=8), :
                ]
            ),
            axis=0,
        )

    nt = (((1,), (1,)), ((), ()))

    def dot_nt(x, y):
        return lax.dot_general(x, y, nt, precision=HIGHEST, preferred_element_type=f32)

    fit_rows = fit_ref.shape[0]
    half = epochs // 2

    @pl.when(is_owner)
    def _():
        pieces = [data(k, t) for k in range(2) for t in range(2)]
        total = sum(dot_nt(d, d) for d in pieces)
        half_sum[...] = total

        def part(which):
            return half_sum.at[pl.ds(pl.multiple_of(which * half, half), half), :]

        pair = remote(part(1 - core), pair_box, pair_sems, partner)
        pair.start()
        pair.wait_recv()
        mine = half_sum[pl.ds(pl.multiple_of(core * half, half), half), :] + pair_box[...]
        slot = gathered.at[me]

        @pl.when(me == root)
        def _():
            gathered[me] = mine

        @pl.when(me != root)
        def _():
            spare[...] = mine
            copy = remote(spare, slot, gather_sems, root)
            copy.start()
            copy.wait_send()

        pair.wait_send()

    @pl.when(me == root)
    def _():
        design_ref[...] = jnp.zeros_like(design_ref)
        known = systematics_ref.shape[1]
        for h in range(2):
            for e in range(local):
                at = (h * local + e) * owners
                design_ref[at : at + owners, 0:known] = systematics_ref[
                    pl.ds(h * owners * local + e, owners, stride=local), :
                ]
        templates = onsets_ref.shape[0]
        lane = iota((epochs, LANES), 1)
        place = iota((epochs, LANES), 0)
        position = lax.rem(place, owners)
        group = place // owners
        epoch = (position + (group // local) * owners) * local + lax.rem(group, local)
        onset = jnp.zeros((epochs, LANES), f32)
        for k in range(templates):
            onset = jnp.where(lane == known + k, onsets_ref[k].astype(f32), onset)
        delay = epoch.astype(f32) - onset
        timescale = (lane - known + 1).astype(f32) * epochs / (2.0 * templates)
        is_template = jnp.logical_and(lane >= known, lane < known + templates)
        timescale = jnp.where(is_template, timescale, 1.0)
        transient = jnp.where(delay >= 0.0, jnp.exp(-jnp.maximum(delay, 0.0) / timescale), 0.0)
        design = jnp.where(is_template, transient, design_ref[...])
        base = dot_nt(design, design)
        diagonal = iota((epochs, LANES), 0) == lane
        base = base + jnp.where(diagonal, cov_ridge, 0.0)

        slots = gathered.at[pl.ds(0, owners - 1)]
        remote(slots, slots, gather_sems, partner).wait_recv()
        total = [jnp.zeros((half, LANES), f32)] * 2
        for c in range(0, owners, 2):
            total = [t + gathered[c + s] for s, t in enumerate(total)]
        scatter = jnp.concatenate(total, axis=0)
        gain = eliminate(base + scatter / pixels, design)
        fit_ref[...] = gain.T[0:fit_rows, :]

        @pl.loop(0, owners)
        def _(step):
            @pl.when(step != me)
            def _():
                remote(fit_ref, fit_ref, (fit_send.at[step], fit_got), step).start()

        projector = jnp.where(diagonal, 1.0, 0.0) - dot_nt(design, gain)
        product = jnp.dot(projector, scatter, precision=HIGHEST, preferred_element_type=f32)
        terms = product * projector
        for h in range(2):
            for e in range(local):
                at = (h * local + e) * owners
                design_ref[pl.ds(h * owners * local + e, owners, stride=local), :] = terms[
                    at : at + owners, :
                ]
        residual = jnp.sum(design_ref[...].T, axis=0, keepdims=True) / pixels
        residual_ref[...] = jnp.broadcast_to(residual, residual_ref.shape)
        scatter_ref[...] = jnp.broadcast_to(residual, scatter_ref.shape)

        @pl.loop(1, devices)
        def _(step):
            other = lax.rem(me + step, devices)
            remote(
                residual_ref, scatter_ref, (residual_send.at[step], residual_got), other
            ).start()

    @pl.when(is_owner)
    def _():
        @pl.when(me != root)
        def _():
            remote(fit_ref, fit_ref, (fit_send.at[0], fit_got), partner).wait_recv()

        def row(k):
            fit = fit_ref[...]
            return jnp.concatenate(
                [
                    jnp.dot(fit, data(k, t), precision=HIGHEST, preferred_element_type=f32)
                    for t in range(2)
                ],
                axis=1,
            )

        coefficients_ref[...] = row(0)
        shifted[0, 0:fit_rows, :] = row(1)
        source = shifted.at[0, pl.ds(0, fit_rows), :]
        copy = remote(source, coefficients_ref, row_sems, me + owners)
        copy.start()
        copy.wait_send()

    @pl.when(jnp.logical_not(is_owner))
    def _():
        remote(coefficients_ref, coefficients_ref, row_sems, partner).wait_recv()

    @pl.when(me != root)
    def _():
        remote(
            residual_ref, scatter_ref, (residual_send.at[0], residual_got), partner
        ).wait_recv()

    @pl.when(me == root)
    def _():
        @pl.loop(0, owners)
        def _(step):
            @pl.when(step != me)
            def _():
                remote(fit_ref, fit_ref, (fit_send.at[step], fit_got), partner).wait_send()

        @pl.loop(1, devices)
        def _(step):
            remote(
                residual_ref, scatter_ref, (residual_send.at[step], residual_got), partner
            ).wait_send()


def shards(
    devices, images, reference_image, kernels, kernel_index, tile_mask, systematics, onsets
):
    local, rows, width = images.shape
    side = kernels.shape[1]
    epochs = systematics.shape[0]
    columns = systematics.shape[1] + onsets.shape[0]
    owners = devices // 2
    vmem = pl.BlockSpec(memory_space=pltpu.VMEM)
    smem = pl.BlockSpec(memory_space=pltpu.SMEM)
    coefficients, scatter = pl.pallas_call(
        functools.partial(body, devices),
        out_shape=(
            jax.ShapeDtypeStruct((columns, width), f32),
            jax.ShapeDtypeStruct((8, epochs), f32),
        ),
        in_specs=[smem, smem, vmem, vmem, vmem, vmem, vmem],
        out_specs=(vmem, vmem),
        scratch_shapes=[
            pltpu.VMEM((local, LANES, LANES), f32),
            pltpu.VMEM((local, side * rows, LANES), bf16),
            pltpu.VMEM((local, side * rows, width), f32),
            pltpu.VMEM((owners * 8, LANES), f32),
            pltpu.VMEM((devices * 8, LANES), f32),
            pltpu.VMEM((epochs // 2, epochs), f32),
            pltpu.VMEM((epochs, epochs), f32),
            pltpu.VMEM((owners, epochs // 2, epochs), f32),
            pltpu.VMEM((columns, epochs), f32),
            pltpu.VMEM((epochs // 2, epochs), f32),
            pltpu.VMEM((8, epochs), f32),
            pltpu.VMEM((epochs, LANES), f32),
            pltpu.SemaphoreType.DMA((8,)),
            pltpu.SemaphoreType.DMA((owners,)),
            pltpu.SemaphoreType.DMA,
            pltpu.SemaphoreType.DMA((devices,)),
            pltpu.SemaphoreType.DMA,
        ],
        compiler_params=pltpu.CompilerParams(collective_id=0, has_side_effects=True),
    )(
        kernel_index,
        onsets,
        images,
        reference_image,
        jnp.transpose(kernels, (1, 0, 2)),
        tile_mask,
        systematics,
    )
    return coefficients[:, None, :], scatter[0]


def solution(mesh):
    in_specs = (
        P(("field", "ep"), None, None),
        P("field", None),
        P(),
        P(("field", "ep")),
        P(("field", "ep"), None, None),
        P("field", None),
        P("field"),
    )
    out_specs = (P(None, ("field", "ep"), None), P("field"))
    return jax.shard_map(
        functools.partial(shards, mesh.shape["ep"]),
        mesh=mesh,
        in_specs=in_specs,
        out_specs=out_specs,
        check_vma=False,
    )
```

time: 701 us -> 104 us (0.15)
  the two profiles are of different devices: /device:TPU:37 before, /device:TPU:1957 now
where the time goes in v1:
time: 104 us; the launch traced here: 103 us
  Pallas kernels  97.9 us (94%)
  local copies, waits for them, and re-layouts  4.78 us (5%)
    pallas_call x1, Pallas kernels, shards(): pl.pallas_call(functools.partial(body, devices), out_shape=(jax.ShapeDtyp...  97.9 us
    unnamed x5, local copies, waits for them, and re-layouts  3.59 us

profile of v1, /device:TPU:1957, one launch (start us, length us, event | category | flops | bytes accessed | tf_op | source)
XLA Modules:
  0.0 103.3 jit_solution(9338274087631123981)
XLA Ops:
  0.6 0.0 copy-start
  0.6 1.4 %copy.9.mask_ref = s32[2,64,2]{2,1,0:T(8,128)} copy(s32[2,64,2]{1,2,0:T(2,128)} %param.11) | data formatting | bytes 2048 | tf_op args[4]
  2.0 0.0 copy-done
  2.0 0.7 copy.10.systematics_ref
  2.8 97.9 %shard_map.86 = (f32[48,256]{1,0:T(8,128)}, f32[8,128]{1,0:T(8,128)}) custom-call(s32[2]{0:T(128)} %index_ref.1, s32[8]{0:T(128)} %onsets_ref.1, f32[2,64,256]{2,1,0:T(8,128)} %images_ref.1, f32[64,256]{1,0:T(8,128)} %reference_ref.1, f32[23,16,23]{2,1,0:T(8,128)} %bitcast.4, s32[2,64,2]{2,1,0:T(8,128)} %copy.9.mask_ref, f32[128,40]{1,0:T(8,128)} %copy.10.systematics_ref), custom_call_target="tpu_custom_call" | custom-call | tf_op jit(solution)/shard_map/pallas_call | solution.py:380
  100.6 1.5 %copy.11 = f32[48,1,256]{2,1,0:T(1,128)} copy(f32[48,1,256]{2,0,1:T(8,128)} %bitcast.5) | data formatting | bytes 98304
  102.1 1.2 %slice_bitcast_fusion = f32[128]{0:T(128)} fusion(f32[8,128]{1,0:T(8,128)} %get-tuple-element.5), kind=kLoop, calls=%fused_computation | loop fusion | bytes 1024 | tf_op jit(solution)/shard_map/squeeze | solution.py:417
Async XLA Ops:
  0.6 1.4 %copy-start = (f32[128,40]{0,1:T(8,128)S(1)}, f32[128,40]{0,1:T(8,128)}, u32[]{:S(2)}) copy-start(f32[128,40]{0,1:T(8,128)} %param.12) | copy-start | bytes 61444

commit v2 on v1

v2 whole, which is shorter than its diff:
```python
import functools

import jax
import jax.numpy as jnp
from jax import lax
from jax.experimental import pallas as pl
from jax.experimental.pallas import tpu as pltpu
from jax.sharding import PartitionSpec as P

f32, bf16, i32 = jnp.float32, jnp.bfloat16, jnp.int32
HIGHEST = lax.Precision.HIGHEST
cov_ridge = 0.5
LANES = 128


def split(x):
    high = x.astype(bf16).astype(f32)
    return high, x - high


def pieces(x):
    high, low = split(x)
    return high.astype(bf16), low.astype(bf16)


def iota(shape, axis):
    return lax.broadcasted_iota(i32, shape, axis)


def correlate(image, kernel, kpad, bands, shifted):
    side = kernel.shape[0]
    half = side // 2
    rows = image.shape[0]
    kpad[...] = jnp.zeros_like(kpad)
    kpad[0:side, 0:side] = kernel
    high, low = split(kpad[...].T)
    base = pltpu.roll(high, LANES - half, 1) + pltpu.roll(low, rows - half, 1)
    lane = iota((rows, LANES), 1)
    band = jnp.abs(lax.rem(lane, rows) - iota((rows, LANES), 0)) <= half
    for b in range(side):
        column = jnp.broadcast_to(base[b : b + 1, :], (rows, LANES))
        column = pltpu.roll(column, 0, 1, stride=1, stride_axis=0)
        bands[b * rows : (b + 1) * rows, :] = jnp.where(band, column, 0.0).astype(bf16)
    high, low = pieces(image)
    left = bands[...]
    shifted[...] = jnp.dot(
        jnp.concatenate([left, left], axis=1),
        jnp.concatenate([high, high, low, low], axis=0),
        preferred_element_type=f32,
    )
    total = [None, None]
    for b in range(side):
        s = b - half
        block = slice(b * rows, (b + 1) * rows)
        first, second = shifted[block, 0:LANES], shifted[block, LANES:]
        if s:
            x = pltpu.roll(first, (-s) % LANES, 1)
            y = pltpu.roll(second, (-s) % LANES, 1)
            if s > 0:
                inside = lane < LANES - s
                first, second = jnp.where(inside, x, y), jnp.where(inside, y, 0.0)
            else:
                inside = lane >= -s
                first, second = jnp.where(inside, x, 0.0), jnp.where(inside, y, x)
        total = [v if t is None else t + v for t, v in zip(total, (first, second))]
    return total


def eliminate(matrix, right):
    count = matrix.shape[0]
    width = 8
    row8 = iota((width, LANES), 0)
    for k in range(0, count, width):
        pivot = slice(k, k + width)
        columns = [
            jnp.broadcast_to(matrix[:, k + j : k + j + 1], (count, LANES)) for j in range(width)
        ]
        block = [c[pivot, :] for c in columns]
        a, x = matrix[pivot, :], right[pivot, :]
        for j in range(width):
            factor = block[j]
            inverse = 1.0 / factor[j : j + 1, :]

            def step(v):
                scaled = v[j : j + 1, :] * inverse
                return jnp.where(row8 == j, scaled, v - factor * scaled)

            a, x = step(a), step(x)
            for m in range(j + 1, width):
                block[m] = step(block[m])

        def update(value, rows):
            for j in range(width):
                value = value - columns[j] * rows[j : j + 1, :]
            above = [value[:k, :]] if k else []
            below = [value[k + width :, :]] if k + width < count else []
            return jnp.concatenate([*above, rows, *below], axis=0)

        if k + width < count:
            matrix = update(matrix, a)
        right = update(right, x)
    return right


NT = (((1,), (1,)), ((), ()))


def dot_nt(x, y):
    return lax.dot_general(x, y, NT, precision=HIGHEST, preferred_element_type=f32)


def gram(x):
    high, low = pieces(x)
    left = jnp.concatenate([high, high, low], axis=1)
    right = jnp.concatenate([high, low, high], axis=1)
    return lax.dot_general(left, right, NT, preferred_element_type=f32)


def fold(value):
    tiles = LANES // 8
    lane = iota((8, LANES), 1)
    block = [value[8 * i : 8 * i + 8, :] for i in range(tiles)]
    folded, last = [], jnp.zeros((8, LANES), f32)
    for i in range(tiles // 2):
        other = block[tiles - 1 - i]
        moved = pltpu.roll(other, 8 * i, 1) if i else other
        folded.append(jnp.where(lane >= 8 * i, block[i], moved))
        last = jnp.where(lane // 8 == tiles - 1 - i, other, last)
    return [*folded, last]


def unfold(folded):
    tiles = LANES // 8
    lane = iota((8, LANES), 1)
    above, blocks = [None] * tiles, [None] * tiles
    for i in range(tiles // 2):
        other = tiles - 1 - i
        moved = pltpu.roll(folded[i], LANES - 8 * i, 1) if i else folded[i]
        above[i] = jnp.where(lane >= 8 * i + 8, folded[i], 0.0)
        above[other] = jnp.where(lane >= 8 * other + 8, moved, 0.0)
        blocks[i] = jnp.where(lane // 8 == i, folded[i], 0.0)
        blocks[other] = jnp.where(lane // 8 == other, folded[-1], 0.0)
    above = jnp.concatenate(above, axis=0)
    return above + above.T + jnp.concatenate(blocks, axis=0)


def body(
    devices,
    index_ref,
    onsets_ref,
    images_ref,
    reference_ref,
    kernels_ref,
    mask_ref,
    systematics_ref,
    coefficients_ref,
    residual_ref,
    kpad,
    bands,
    shifted,
    parcel,
    inbox,
    relay,
    folded_ref,
    pair_box,
    sum_ref,
    gathered,
    fit_ref,
    row_ref,
    mask_pad,
    design_ref,
    sems,
    parcel_send,
    relay_send,
    relay_got,
    fit_send,
    residual_send,
):
    local, rows, width = images_ref.shape
    epochs = systematics_ref.shape[1]
    owners = devices // 2
    near = owners // 2
    root = 1
    pixels = float(rows * width)
    me = lax.axis_index("ep")
    core = lax.rem(me, 2)
    partner = me + 1 - 2 * core
    is_owner = me < owners
    is_late = jnp.logical_not(is_owner)

    def remote(source, target, send, receive, device):
        return pltpu.make_async_remote_copy(
            src_ref=source,
            dst_ref=target,
            send_sem=send,
            recv_sem=receive,
            device_id={"ep": device},
        )

    def tile(ref, index):
        return ref.at[pl.ds(pl.multiple_of(index * 8, 8), 8), :]

    def relayed(owner, late):
        return jnp.logical_and(owner >= near, owner // 2 <= late // 2 - near)

    barrier = pltpu.get_barrier_semaphore()

    @pl.when(is_owner)
    def _():
        @pl.loop(1, devices)
        def _(step):
            other = lax.rem(me + step, devices)

            @pl.when(jnp.logical_not(jnp.logical_and(other >= owners, relayed(me, other))))
            def _():
                pl.semaphore_signal(barrier, inc=1, device_id={"ep": other})

    mask_pad[...] = jnp.zeros_like(mask_pad)
    halves = width // LANES
    for e in range(local):
        mask_pad[e * halves : (e + 1) * halves, 0:rows] = mask_ref[e].astype(f32)
    mask = mask_pad[...].T

    for e in range(local):
        conv = correlate(
            images_ref[e], kernels_ref[:, index_ref[e], :], kpad.at[e], bands.at[e], shifted.at[e]
        )
        for t in range(halves):
            lanes = slice(t * LANES, (t + 1) * LANES)
            column = e * halves + t
            good = jnp.broadcast_to(mask[0:rows, column : column + 1], (rows, LANES))
            difference = (reference_ref[:, lanes] - conv[t]) * good
            parcel[pl.ds(t * 2 + e, owners, stride=8), :] = difference[:owners, :]
            parcel[pl.ds(4 + t * 2 + e, near, stride=8), :] = difference[owners + near :, :]
            parcel[pl.ds(near * 8 + 4 + t * 2 + e, near, stride=8), :] = difference[
                owners : owners + near, :
            ]

    served = owners + lax.rem(me + near, owners)
    got_parcel = sems.at[0]

    @pl.when(is_owner)
    def _():
        pl.semaphore_wait(barrier, owners - 1)

    @pl.when(is_late)
    def _():
        direct = jnp.minimum(near // 2, devices // 2 - 1 - me // 2)
        pl.semaphore_wait(barrier, near + 2 * direct)

    for owner in reversed(range(owners)):
        source = parcel.at[pl.ds(owner * 8, 8), :]
        through = jnp.logical_and(is_late, relayed(owner, me)) if owner >= near else False

        def direct(owner=owner, source=source):
            remote(source, tile(inbox, me), parcel_send, got_parcel, owner).start()

        if owner >= near:

            @pl.when(through)
            def _(owner=owner, source=source):
                place = me - (owners + near)
                target = tile(relay, place)
                remote(source, target, parcel_send, relay_got.at[place], owner - near).start()

        @pl.when(jnp.logical_and(owner != me, jnp.logical_not(through)))
        def _(direct=direct):
            direct()

    @pl.when(me < near)
    def _():
        @pl.loop(0, near)
        def _(step):
            place = near - 1 - step
            late = place + owners + near

            @pl.when(relayed(me + near, late))
            def _():
                slot = tile(relay, place)
                remote(slot, slot, parcel_send, relay_got.at[place], partner).wait_recv()
                target = tile(inbox, late)
                remote(slot, target, relay_send.at[place], got_parcel, me + near).start()

    @pl.when(is_owner)
    def _():
        mine = pl.ds(pl.multiple_of(me * 8, 8), 8)
        inbox[mine, :] = parcel[mine, :]
        arrived = inbox.at[pl.ds(0, (devices - 1) * 8), :]
        remote(arrived, arrived, parcel_send, got_parcel, partner).wait_recv()

    def data(k, t):
        return jnp.concatenate(
            [
                inbox[pl.ds(h * owners * 8 + k * 4 + t * 2 + e, owners, stride=8), :]
                for h in range(2)
                for e in range(local)
            ],
            axis=0,
        )

    fit_rows = fit_ref.shape[0]
    share = pair_box.shape[0]

    pair_send, pair_got, gather_send, gather_got = (sems.at[i] for i in range(1, 5))
    fit_got, row_send, row_got, residual_got, pass_send = (sems.at[i] for i in range(5, 10))

    def part(which):
        return folded_ref.at[pl.ds(pl.multiple_of(which * share, 8), share), :]

    pair = remote(part(1 - core), pair_box, pair_send, pair_got, partner)
    to_root = remote(sum_ref, gathered.at[me], gather_send, gather_got, root)

    @pl.when(is_owner)
    def _():
        total = gram(jnp.concatenate([data(k, t) for k in range(2) for t in range(halves)], axis=1))
        tiles = fold(total)
        folded_ref[...] = jnp.zeros_like(folded_ref)
        for i, value in enumerate(tiles):
            folded_ref[i * 8 : i * 8 + 8, :] = value
        pair.start()
        pair.wait_recv()
        mine = folded_ref[pl.ds(pl.multiple_of(core * share, 8), share), :] + pair_box[...]

        @pl.when(me == root)
        def _():
            gathered[me] = mine

        @pl.when(me != root)
        def _():
            sum_ref[...] = mine
            to_root.start()

    @pl.when(me == root)
    def _():
        known = systematics_ref.shape[0]
        templates = onsets_ref.shape[0]
        design_ref[...] = jnp.zeros_like(design_ref)
        design_ref[0:known, :] = systematics_ref[...]
        design_ref[...] = design_ref[...].T
        design = jnp.concatenate(
            [
                design_ref[pl.ds(h * owners * local + e, owners, stride=local), :]
                for h in range(2)
                for e in range(local)
            ],
            axis=0,
        )
        lane = iota((epochs, LANES), 1)
        place = iota((epochs, LANES), 0)
        group = place // owners
        epoch = lax.rem(place, owners) * local + (group // local) * owners * local
        epoch = epoch + lax.rem(group, local)
        onset = jnp.zeros((epochs, LANES), f32)
        for k in range(templates):
            onset = jnp.where(lane == known + k, onsets_ref[k].astype(f32), onset)
        delay = epoch.astype(f32) - onset
        timescale = (lane - known + 1).astype(f32) * epochs / (2.0 * templates)
        is_template = jnp.logical_and(lane >= known, lane < known + templates)
        timescale = jnp.where(is_template, timescale, 1.0)
        transient = jnp.where(delay >= 0.0, jnp.exp(-jnp.maximum(delay, 0.0) / timescale), 0.0)
        design = jnp.where(is_template, transient, design)
        base = dot_nt(design, design)
        diagonal = place == lane
        base = base + jnp.where(diagonal, cov_ridge, 0.0)

        slots = gathered.at[pl.ds(0, owners - 1)]
        remote(slots, slots, gather_send, gather_got, partner).wait_recv()
        total = [gathered[0], gathered[1]]
        for c in range(2, owners, 2):
            total = [t + gathered[c + s] for s, t in enumerate(total)]
        total = jnp.concatenate(total, axis=0)
        scatter = unfold([total[8 * i : 8 * i + 8, :] for i in range(LANES // 16 + 1)])
        gain = eliminate(base + scatter / pixels, design)
        fit_ref[...] = gain.T[0:fit_rows, :]

        for other in range(owners):
            if other != root:
                remote(fit_ref, fit_ref, fit_send.at[other], fit_got, other).start()

        projector = jnp.where(diagonal, 1.0, 0.0) - dot_nt(design, gain)
        product = jnp.dot(projector, scatter, precision=HIGHEST, preferred_element_type=f32)
        terms = product * projector
        for h in range(2):
            for e in range(local):
                at = (h * local + e) * owners
                design_ref[pl.ds(h * owners * local + e, owners, stride=local), :] = terms[
                    at : at + owners, :
                ]
        residual = jnp.sum(design_ref[...].T, axis=0, keepdims=True) / pixels
        residual_ref[...] = jnp.broadcast_to(residual, residual_ref.shape)
        for other in range(owners):
            if other != root:
                remote(
                    residual_ref, residual_ref, residual_send.at[other], residual_got, other
                ).start()

    def row(k):
        fit = fit_ref[...]
        return jnp.concatenate(
            [
                jnp.dot(fit, data(k, t), precision=HIGHEST, preferred_element_type=f32)
                for t in range(halves)
            ],
            axis=1,
        )

    fit_here = remote(fit_ref, fit_ref, fit_send.at[0], fit_got, partner)
    residual_here = remote(residual_ref, residual_ref, pass_send, residual_got, served)
    row_out = remote(row_ref, coefficients_ref, row_send, row_got, served)

    @pl.when(is_owner)
    def _():
        @pl.when(me != root)
        def _():
            fit_here.wait_recv()

        coefficients_ref[...] = row(0)
        row_ref[...] = row(1)
        row_out.start()

        @pl.when(me != root)
        def _():
            residual_here.wait_recv()

        residual_here.start()

        sent = parcel.at[pl.ds(0, (owners - 1) * 8), :]
        remote(sent, sent, parcel_send, got_parcel, partner).wait_send()

        @pl.when(me < near)
        def _():
            @pl.loop(0, near)
            def _(place):
                @pl.when(relayed(me + near, place + owners + near))
                def _():
                    slot = tile(relay, place)
                    remote(slot, slot, relay_send.at[place], got_parcel, partner).wait_send()

        pair.wait_send()

        @pl.when(me != root)
        def _():
            to_root.wait_send()

        row_out.wait_send()
        residual_here.wait_send()

    @pl.when(is_late)
    def _():
        remote(parcel, parcel, parcel_send, got_parcel, partner).wait_send()
        row_out.wait_recv()
        residual_here.wait_recv()

    @pl.when(me == root)
    def _():
        for other in range(owners):
            if other != root:
                remote(fit_ref, fit_ref, fit_send.at[other], fit_got, other).wait_send()
                remote(
                    residual_ref, residual_ref, residual_send.at[other], residual_got, other
                ).wait_send()


def finish(coefficients_ref, residual_ref, first_ref, second_ref):
    first_ref[...] = coefficients_ref[...].reshape(first_ref.shape)
    second_ref[...] = residual_ref[0]


def shards(
    devices, images, reference_image, kernels, kernel_index, tile_mask, systematics, onsets
):
    local, rows, width = images.shape
    side = kernels.shape[1]
    epochs = systematics.shape[0]
    columns = systematics.shape[1] + onsets.shape[0]
    owners = devices // 2
    near = owners // 2
    share = LANES // 8 // 4 * 8 + 8
    vmem = pl.BlockSpec(memory_space=pltpu.VMEM)
    smem = pl.BlockSpec(memory_space=pltpu.SMEM)
    dma = pltpu.SemaphoreType.DMA
    coefficients, residual = pl.pallas_call(
        functools.partial(body, devices),
        out_shape=(
            jax.ShapeDtypeStruct((columns, width), f32),
            jax.ShapeDtypeStruct((8, epochs), f32),
        ),
        in_specs=[smem, smem, vmem, vmem, vmem, vmem, vmem],
        out_specs=(vmem, vmem),
        scratch_shapes=[
            pltpu.VMEM((local, LANES, LANES), f32),
            pltpu.VMEM((local, side * rows, LANES), bf16),
            pltpu.VMEM((local, side * rows, width), f32),
            pltpu.VMEM((owners * 8, LANES), f32),
            pltpu.VMEM((devices * 8, LANES), f32),
            pltpu.VMEM((near * 8, LANES), f32),
            pltpu.VMEM((2 * share, epochs), f32),
            pltpu.VMEM((share, epochs), f32),
            pltpu.VMEM((share, epochs), f32),
            pltpu.VMEM((owners, share, epochs), f32),
            pltpu.VMEM((columns, epochs), f32),
            pltpu.VMEM((columns, width), f32),
            pltpu.VMEM((8, LANES), f32),
            pltpu.VMEM((epochs, LANES), f32),
            dma((10,)),
            dma,
            dma((near,)),
            dma((near,)),
            dma((owners,)),
            dma((owners,)),
        ],
        compiler_params=pltpu.CompilerParams(collective_id=0, has_side_effects=True),
    )(
        kernel_index,
        onsets,
        images,
        reference_image,
        jnp.transpose(kernels, (1, 0, 2)),
        jnp.transpose(tile_mask, (0, 2, 1)),
        systematics.T,
    )
    return pl.pallas_call(
        finish,
        out_shape=(
            jax.ShapeDtypeStruct((columns, 1, width), f32),
            jax.ShapeDtypeStruct((epochs,), f32),
        ),
        in_specs=[vmem, vmem],
        out_specs=(vmem, vmem),
    )(coefficients, residual)


def solution(mesh):
    in_specs = (
        P(("field", "ep"), None, None),
        P("field", None),
        P(),
        P(("field", "ep")),
        P(("field", "ep"), None, None),
        P("field", None),
        P("field"),
    )
    out_specs = (P(None, ("field", "ep"), None), P("field"))
    return jax.shard_map(
        functools.partial(shards, mesh.shape["ep"]),
        mesh=mesh,
        in_specs=in_specs,
        out_specs=out_specs,
        check_vma=False,
    )
```

time: 104 us -> 96.1 us (0.924)
  the two profiles are of different devices: /device:TPU:1957 before, /device:TPU:37 now
where the time goes in v2:
time: 96.1 us; the launch traced here: 95.4 us
  Pallas kernels  94.7 us (99%)
    pallas_call x1, Pallas kernels, shards(): pl.pallas_call(functools.partial(body, devices), out_shape=(jax.ShapeDtyp...  93.3 us

profile of v2, /device:TPU:37, one launch (start us, length us, event | category | flops | bytes accessed | tf_op | source)
XLA Modules:
  0.0 95.4 jit_solution(15112117955580614505)
XLA Ops:
  0.6 93.3 %shard_map.86 = (f32[48,256]{1,0:T(8,128)}, f32[8,128]{1,0:T(8,128)}) custom-call(s32[2]{0:T(128)} %index_ref.1, s32[8]{0:T(128)} %onsets_ref.1, f32[2,64,256]{2,1,0:T(8,128)} %images_ref.1, f32[64,256]{1,0:T(8,128)} %reference_ref.1, f32[23,16,23]{2,1,0:T(8,128)} %bitcast.3, s32[2,2,64]{2,1,0:T(2,128)} %bitcast.5, f32[40,128]{1,0:T(8,128)} %bitcast.4), custom_call_target="tpu_custom_call" | custom-call | tf_op jit(solution)/shard_map/pallas_call | solution.py:482
  93.9 1.4 %shard_map.87 = (f32[48,1,256]{2,1,0:T(1,128)}, f32[128]{0:T(128)}) custom-call(f32[48,256]{1,0:T(8,128)} %get-tuple-element.4.coefficients_ref, f32[8,128]{1,0:T(8,128)} %get-tuple-element.5.residual_ref), custom_call_target="tpu_custom_call" | custom-call | tf_op jit(solution)/shard_map/pallas_call | solution.py:522

commit v3 on v2

v3 whole, which is shorter than its diff:
```python
import functools

import jax
import jax.numpy as jnp
from jax import lax
from jax.experimental import pallas as pl
from jax.experimental.pallas import tpu as pltpu
from jax.sharding import PartitionSpec as P

f32, bf16, i32 = jnp.float32, jnp.bfloat16, jnp.int32
HIGHEST = lax.Precision.HIGHEST
cov_ridge = 0.5
LANES = 128


def split(x):
    high = x.astype(bf16).astype(f32)
    return high, x - high


def pieces(x):
    high, low = split(x)
    return high.astype(bf16), low.astype(bf16)


def iota(shape, axis):
    return lax.broadcasted_iota(i32, shape, axis)


def correlate(image, kernel, kpad, bands, shifted):
    side = kernel.shape[0]
    half = side // 2
    rows = image.shape[0]
    kpad[...] = jnp.zeros_like(kpad)
    kpad[0:side, 0:side] = kernel
    high, low = split(kpad[...].T)
    base = pltpu.roll(high, LANES - half, 1) + pltpu.roll(low, rows - half, 1)
    lane = iota((rows, LANES), 1)
    band = jnp.abs(lax.rem(lane, rows) - iota((rows, LANES), 0)) <= half
    for b in range(side):
        column = jnp.broadcast_to(base[b : b + 1, :], (rows, LANES))
        column = pltpu.roll(column, 0, 1, stride=1, stride_axis=0)
        bands[b * rows : (b + 1) * rows, :] = jnp.where(band, column, 0.0).astype(bf16)
    high, low = pieces(image)
    left = bands[...]
    shifted[...] = jnp.dot(
        jnp.concatenate([left, left], axis=1),
        jnp.concatenate([high, high, low, low], axis=0),
        preferred_element_type=f32,
    )
    total = [None, None]
    for b in range(side):
        s = b - half
        block = slice(b * rows, (b + 1) * rows)
        first, second = shifted[block, 0:LANES], shifted[block, LANES:]
        if s:
            x = pltpu.roll(first, (-s) % LANES, 1)
            y = pltpu.roll(second, (-s) % LANES, 1)
            if s > 0:
                inside = lane < LANES - s
                first, second = jnp.where(inside, x, y), jnp.where(inside, y, 0.0)
            else:
                inside = lane >= -s
                first, second = jnp.where(inside, x, 0.0), jnp.where(inside, y, x)
        total = [v if t is None else t + v for t, v in zip(total, (first, second))]
    return total


def eliminate(matrix, right):
    count = matrix.shape[0]
    width = 8
    row8 = iota((width, LANES), 0)
    for k in range(0, count, width):
        pivot = slice(k, k + width)
        columns = [
            jnp.broadcast_to(matrix[:, k + j : k + j + 1], (count, LANES)) for j in range(width)
        ]
        block = [c[pivot, :] for c in columns]
        a, x = matrix[pivot, :], right[pivot, :]
        for j in range(width):
            factor = block[j]
            inverse = 1.0 / factor[j : j + 1, :]

            def step(v):
                scaled = v[j : j + 1, :] * inverse
                return jnp.where(row8 == j, scaled, v - factor * scaled)

            a, x = step(a), step(x)
            for m in range(j + 1, width):
                block[m] = step(block[m])

        def update(value, rows):
            for j in range(width):
                value = value - columns[j] * rows[j : j + 1, :]
            above = [value[:k, :]] if k else []
            below = [value[k + width :, :]] if k + width < count else []
            return jnp.concatenate([*above, rows, *below], axis=0)

        if k + width < count:
            matrix = update(matrix, a)
        right = update(right, x)
    return right


NT = (((1,), (1,)), ((), ()))


def dot_nt(x, y):
    return lax.dot_general(x, y, NT, precision=HIGHEST, preferred_element_type=f32)


def gram(x):
    high, low = pieces(x)
    left = jnp.concatenate([high, high, low], axis=1)
    right = jnp.concatenate([high, low, high], axis=1)
    return lax.dot_general(left, right, NT, preferred_element_type=f32)


def fold(value):
    tiles = LANES // 8
    lane = iota((8, LANES), 1)
    block = [value[8 * i : 8 * i + 8, :] for i in range(tiles)]
    folded, last = [], jnp.zeros((8, LANES), f32)
    for i in range(tiles // 2):
        other = block[tiles - 1 - i]
        moved = pltpu.roll(other, 8 * i, 1) if i else other
        folded.append(jnp.where(lane >= 8 * i, block[i], moved))
        last = jnp.where(lane // 8 == tiles - 1 - i, other, last)
    return [*folded, last]


def unfold(folded):
    tiles = LANES // 8
    lane = iota((8, LANES), 1)
    above, blocks = [None] * tiles, [None] * tiles
    for i in range(tiles // 2):
        other = tiles - 1 - i
        moved = pltpu.roll(folded[i], LANES - 8 * i, 1) if i else folded[i]
        above[i] = jnp.where(lane >= 8 * i + 8, folded[i], 0.0)
        above[other] = jnp.where(lane >= 8 * other + 8, moved, 0.0)
        blocks[i] = jnp.where(lane // 8 == i, folded[i], 0.0)
        blocks[other] = jnp.where(lane // 8 == other, folded[-1], 0.0)
    above = jnp.concatenate(above, axis=0)
    return above + above.T + jnp.concatenate(blocks, axis=0)


def body(
    devices,
    index_ref,
    onsets_ref,
    images_hbm,
    reference_hbm,
    kernels_hbm,
    mask_hbm,
    systematics_hbm,
    coefficients_ref,
    residual_ref,
    images_ref,
    reference_ref,
    kernels_ref,
    mask_ref,
    systematics_ref,
    kpad,
    bands,
    shifted,
    parcel,
    inbox,
    relay_up,
    relay_down,
    folded_ref,
    pair_box,
    sum_ref,
    gathered,
    fit_ref,
    mask_pad,
    design_ref,
    load_sems,
    sems,
    fit_send,
    residual_send,
):
    local, rows, width = images_ref.shape
    epochs = systematics_ref.shape[1]
    halves = width // LANES
    root = 1
    pixels = float(rows * width)
    chips = devices // 2
    reach = chips // 4
    me = lax.axis_index("ep")
    core = lax.rem(me, 2)
    chip = me // 2
    partner = me + 1 - 2 * core

    def remote(source, target, send, receive, device):
        return pltpu.make_async_remote_copy(
            src_ref=source,
            dst_ref=target,
            send_sem=send,
            recv_sem=receive,
            device_id={"ep": device},
        )

    def at(offset, which):
        return lax.rem(chip + offset + chips, chips) * 2 + which

    close = [d * sign for d in range(reach, 0, -1) for sign in (1, -1)]

    barrier = pltpu.get_barrier_semaphore()
    for offset in close:
        for which in range(2):
            pl.semaphore_signal(barrier, inc=1, device_id={"ep": at(offset, which)})
    pl.semaphore_signal(barrier, inc=1, device_id={"ep": partner})

    loads = [
        pltpu.make_async_copy(source, target, load_sems.at[i])
        for i, (source, target) in enumerate(
            (
                (kernels_hbm, kernels_ref),
                (images_hbm, images_ref),
                (mask_hbm, mask_ref),
                (reference_hbm, reference_ref),
                (systematics_hbm, systematics_ref),
            )
        )
    ]
    for load in loads:
        load.start()
    for load in loads:
        load.wait()

    mask_pad[...] = jnp.zeros_like(mask_pad)
    for e in range(local):
        mask_pad[e * halves : (e + 1) * halves, 0:rows] = mask_ref[e].astype(f32)
    mask = mask_pad[...].T

    for e in range(local):
        conv = correlate(
            images_ref[e], kernels_ref[:, index_ref[e], :], kpad.at[e], bands.at[e], shifted.at[e]
        )
        for t in range(halves):
            lanes = slice(t * LANES, (t + 1) * LANES)
            line = e * halves + t
            good = jnp.broadcast_to(mask[0:rows, line : line + 1], (rows, LANES))
            parcel[:, line, :] = (reference_ref[:, lanes] - conv[t]) * good

    (
        parcel_send,
        got_piece,
        up_got,
        down_got,
        pass_send,
        pair_send,
        pair_got,
        gather_send,
        gather_got,
        fit_got,
        residual_got,
    ) = (sems.at[i] for i in range(11))

    pl.semaphore_wait(barrier, 4 * reach + 1)

    far = [(relay_up, up_got, reach, 1, chips // 2 - reach)]
    far.append((relay_down, down_got, -reach, -1, chips // 2 - reach - 1))
    for step in range(chips // 2 - reach, 0, -1):
        for box, got, first, sign, count in far:
            for which in range(2):
                if step <= count:
                    piece = parcel.at[at(first + sign * step, which)]
                    slot = box.at[2 * (step - 1) + which]
                    remote(piece, slot, parcel_send, got, at(first, core)).start()
    for offset in close:
        for which in range(2):
            other = at(offset, which)
            remote(parcel.at[other], inbox.at[me], parcel_send, got_piece, other).start()
    remote(parcel.at[partner], inbox.at[me], parcel_send, got_piece, partner).start()
    inbox[me] = parcel[me]
    for box, got, first, sign, count in far:
        remote(box, box, parcel_send, got, partner).wait_recv()
        for step in range(count, 0, -1):
            for which in range(2):
                target = inbox.at[at(-first, core)]
                piece = box.at[2 * (step - 1) + which]
                remote(piece, target, pass_send, got_piece, at(sign * step, which)).start()
    arrived = inbox.at[pl.ds(0, devices - 1)]
    remote(arrived, arrived, parcel_send, got_piece, partner).wait_recv()

    def data(t):
        return jnp.concatenate([inbox[:, e * halves + t, :] for e in range(local)], axis=0)

    fit_rows = fit_ref.shape[0]
    share = pair_box.shape[0]

    def part(which):
        return folded_ref.at[pl.ds(pl.multiple_of(which * share, 8), share), :]

    pair = remote(part(1 - core), pair_box, pair_send, pair_got, partner)
    to_root = remote(sum_ref, gathered.at[me], gather_send, gather_got, root)
    tiles = fold(gram(jnp.concatenate([data(t) for t in range(halves)], axis=1)))
    folded_ref[...] = jnp.zeros_like(folded_ref)
    for i, value in enumerate(tiles):
        folded_ref[i * 8 : i * 8 + 8, :] = value
    pair.start()
    pair.wait_recv()
    mine = folded_ref[pl.ds(pl.multiple_of(core * share, 8), share), :] + pair_box[...]

    @pl.when(me == root)
    def _():
        gathered[me] = mine

    @pl.when(me != root)
    def _():
        sum_ref[...] = mine
        to_root.start()

    @pl.when(me == root)
    def _():
        known = systematics_ref.shape[0]
        templates = onsets_ref.shape[0]
        design_ref[...] = jnp.zeros_like(design_ref)
        design_ref[0:known, :] = systematics_ref[...]
        design_ref[...] = design_ref[...].T
        design = jnp.concatenate(
            [design_ref[pl.ds(e, devices, stride=local), :] for e in range(local)], axis=0
        )
        lane = iota((epochs, LANES), 1)
        place = iota((epochs, LANES), 0)
        epoch = lax.rem(place, devices) * local + place // devices
        onset = jnp.zeros((epochs, LANES), f32)
        for k in range(templates):
            onset = jnp.where(lane == known + k, onsets_ref[k].astype(f32), onset)
        delay = epoch.astype(f32) - onset
        timescale = (lane - known + 1).astype(f32) * epochs / (2.0 * templates)
        is_template = jnp.logical_and(lane >= known, lane < known + templates)
        timescale = jnp.where(is_template, timescale, 1.0)
        transient = jnp.where(delay >= 0.0, jnp.exp(-jnp.maximum(delay, 0.0) / timescale), 0.0)
        design = jnp.where(is_template, transient, design)
        base = dot_nt(design, design)
        diagonal = place == lane
        base = base + jnp.where(diagonal, cov_ridge, 0.0)

        slots = gathered.at[pl.ds(0, devices - 1)]
        remote(slots, slots, gather_send, gather_got, partner).wait_recv()
        total = [gathered[0], gathered[1]]
        for c in range(2, devices, 2):
            total = [t + gathered[c + s] for s, t in enumerate(total)]
        total = jnp.concatenate(total, axis=0)
        scatter = unfold([total[8 * i : 8 * i + 8, :] for i in range(LANES // 16 + 1)])
        gain = eliminate(base + scatter / pixels, design)
        fit_ref[...] = gain.T[0:fit_rows, :]

        fits = []
        for offset in range(chips // 2 + 1):
            for other in ((offset, chips - offset) if 0 < offset < chips // 2 else (offset,)):
                fits += [2 * other + which for which in range(2) if 2 * other + which != root]
        for other in fits:
            remote(fit_ref, fit_ref, fit_send.at[other], fit_got, other).start()

        projector = jnp.where(diagonal, 1.0, 0.0) - dot_nt(design, gain)
        product = jnp.dot(projector, scatter, precision=HIGHEST, preferred_element_type=f32)
        terms = product * projector
        for e in range(local):
            design_ref[pl.ds(e, devices, stride=local), :] = terms[
                e * devices : (e + 1) * devices, :
            ]
        residual = jnp.sum(design_ref[...].T, axis=0, keepdims=True) / pixels
        residual_ref[...] = jnp.broadcast_to(residual, residual_ref.shape)
        for other in fits:
            remote(
                residual_ref, residual_ref, residual_send.at[other], residual_got, other
            ).start()

    fit_here = remote(fit_ref, fit_ref, parcel_send, fit_got, partner)
    residual_here = remote(residual_ref, residual_ref, parcel_send, residual_got, partner)

    @pl.when(me != root)
    def _():
        fit_here.wait_recv()

    for t in range(halves):
        coefficients_ref[:, t * LANES : (t + 1) * LANES] = jnp.dot(
            fit_ref[...], data(t), precision=HIGHEST, preferred_element_type=f32
        )

    sent = inbox.at[pl.ds(0, devices - 1)]
    remote(sent, sent, parcel_send, got_piece, partner).wait_send()
    for box, got, first, sign, count in far:
        remote(box, box, pass_send, got, partner).wait_send()
    pair.wait_send()

    @pl.when(me != root)
    def _():
        to_root.wait_send()
        residual_here.wait_recv()

    @pl.when(me == root)
    def _():
        for other in range(devices):
            if other != root:
                remote(fit_ref, fit_ref, fit_send.at[other], fit_got, other).wait_send()
                remote(
                    residual_ref, residual_ref, residual_send.at[other], residual_got, other
                ).wait_send()


def finish(coefficients_ref, residual_ref, first_ref, second_ref):
    first_ref[...] = coefficients_ref[...].reshape(first_ref.shape)
    second_ref[...] = residual_ref[0]


def shards(
    devices, images, reference_image, kernels, kernel_index, tile_mask, systematics, onsets
):
    local, rows, width = images.shape
    side = kernels.shape[1]
    epochs = systematics.shape[0]
    columns = systematics.shape[1] + onsets.shape[0]
    lines = local * width // LANES
    reach = devices // 8
    share = LANES // 8 // 4 * 8 + 8
    vmem = pl.BlockSpec(memory_space=pltpu.VMEM)
    smem = pl.BlockSpec(memory_space=pltpu.SMEM)
    anywhere = pl.BlockSpec(memory_space=pl.ANY)
    dma = pltpu.SemaphoreType.DMA
    inputs = (
        images,
        reference_image,
        jnp.transpose(kernels, (1, 0, 2)),
        jnp.transpose(tile_mask, (0, 2, 1)),
        systematics.T,
    )
    coefficients, residual = pl.pallas_call(
        functools.partial(body, devices),
        out_shape=(
            jax.ShapeDtypeStruct((columns, width), f32),
            jax.ShapeDtypeStruct((8, epochs), f32),
        ),
        in_specs=[smem, smem] + [anywhere] * len(inputs),
        out_specs=(vmem, vmem),
        scratch_shapes=[pltpu.VMEM(x.shape, x.dtype) for x in inputs]
        + [
            pltpu.VMEM((local, LANES, LANES), f32),
            pltpu.VMEM((local, side * rows, LANES), bf16),
            pltpu.VMEM((local, side * rows, width), f32),
            pltpu.VMEM((devices, lines, LANES), f32),
            pltpu.VMEM((devices, lines, LANES), f32),
            pltpu.VMEM((2 * reach, lines, LANES), f32),
            pltpu.VMEM((2 * reach - 2, lines, LANES), f32),
            pltpu.VMEM((2 * share, epochs), f32),
            pltpu.VMEM((share, epochs), f32),
            pltpu.VMEM((share, epochs), f32),
            pltpu.VMEM((devices, share, epochs), f32),
            pltpu.VMEM((columns, epochs), f32),
            pltpu.VMEM((8, LANES), f32),
            pltpu.VMEM((epochs, LANES), f32),
            dma((len(inputs),)),
            dma((11,)),
            dma((devices,)),
            dma((devices,)),
        ],
        compiler_params=pltpu.CompilerParams(collective_id=0, has_side_effects=True),
    )(kernel_index, onsets, *inputs)
    return pl.pallas_call(
        finish,
        out_shape=(
            jax.ShapeDtypeStruct((columns, 1, width), f32),
            jax.ShapeDtypeStruct((epochs,), f32),
        ),
        in_specs=[vmem, vmem],
        out_specs=(vmem, vmem),
    )(coefficients, residual)


def solution(mesh):
    in_specs = (
        P(("field", "ep"), None, None),
        P("field", None),
        P(),
        P(("field", "ep")),
        P(("field", "ep"), None, None),
        P("field", None),
        P("field"),
    )
    out_specs = (P(None, ("field", "ep"), None), P("field"))
    return jax.shard_map(
        functools.partial(shards, mesh.shape["ep"]),
        mesh=mesh,
        in_specs=in_specs,
        out_specs=out_specs,
        check_vma=False,
    )
```

time: 96.1 us -> 81.1 us (0.84)
  Pallas kernels: 94.7 us -> 80.3 us
    pallas_call x1, Pallas kernels: 93.3 us -> 78.8 us  [shards(): pl.pallas_call(functools.partial(body, devices), out_shape=(jax.ShapeDtyp...]
where the time goes in v3:
time: 81.1 us; the launch traced here: 80.9 us
  Pallas kernels  80.3 us (99%)
    pallas_call x1, Pallas kernels, shards(): pl.pallas_call(functools.partial(body, devices), out_shape=(jax.ShapeDtyp...  78.8 us

profile of v3, /device:TPU:37, one launch (start us, length us, event | category | flops | bytes accessed | tf_op | source)
XLA Modules:
  0.0 80.9 jit_solution(14422935795968269668)
XLA Ops:
  0.6 78.8 %shard_map.86 = (f32[48,256]{1,0:T(8,128)}, f32[8,128]{1,0:T(8,128)}) custom-call(s32[2]{0:T(128)} %index_ref.1, s32[8]{0:T(128)} %onsets_ref.1, f32[2,64,256]{2,1,0:T(8,128)} %images_hbm.1, f32[64,256]{1,0:T(8,128)} %reference_hbm.1, f32[23,16,23]{2,1,0:T(8,128)} %bitcast.3, s32[2,2,64]{2,1,0:T(2,128)} %bitcast.5, f32[40,128]{1,0:T(8,128)} %bitcast.4), custom_call_target="tpu_custom_call" | custom-call | tf_op jit(solution)/shard_map/pallas_call | solution.py:431
  79.5 1.4 %shard_map.87 = (f32[48,1,256]{2,1,0:T(1,128)}, f32[128]{0:T(128)}) custom-call(f32[48,256]{1,0:T(8,128)} %get-tuple-element.4.coefficients_ref, f32[8,128]{1,0:T(8,128)} %get-tuple-element.5.residual_ref), custom_call_target="tpu_custom_call" | custom-call | tf_op jit(solution)/shard_map/pallas_call | solution.py:462
